TPU v7x, 32 devices: a whole 2x2x4 slice. The times are simulated.
32 devices in a mesh: wide: 16 (over z, x, core), pair: 2 (over y).
Axes of the slice: x: 2, y: 2, z: 4, core: 2. Of those that a mesh axis runs over, the one named last changes fastest.
Arguments:
- pooled_b: bfloat16 [32, 16, 512, 128], P('wide', None, 'pair'), may hold values from -6 to 6
- dense_output_second: bfloat16 [8192, 128], P(('wide', 'pair')), may hold values from -4 to 4
- counts_b: int32 [8192, 26], P(('wide', 'pair')), may hold values from 1 to 8
- slot_of: int32 [32], replicated, may hold values from 0 to 31, each once
- stacked_a: bfloat16 [8192, 3456], P(('wide', 'pair')), may hold values from -4 to 4
- upstream_a: bfloat16 [8192, 3456], P(('wide', 'pair')), may hold values from -2 to 2
- counts_a: int32 [8192, 26], P(('wide', 'pair')), may hold values from 1 to 8
- down_projection: bfloat16 [3456, 512], P('wide'), may hold values from -0.109375 to 0.109375
- proj_up: bfloat16 [512, 3456], P(None, 'wide'), may hold values from -0.25 to 0.25
- cross_layer_bias: bfloat16 [3456], P('wide'), may hold values from -3 to 3
Outputs:
- crossed_b: bfloat16 [8192, 3456], P(('wide', 'pair'))
- dense_grad_a: bfloat16 [8192, 128], P(('wide', 'pair'))
- pooled_grad_a: bfloat16 [32, 16, 512, 128], P('wide', None, 'pair')
- grad_down: float32 [3456, 512], P('wide')
- grad_up: float32 [512, 3456], P(None, 'wide')
- grad_bias: float32 [3456], P('wide')
Inputs may be any that keep to these rules, and one draw needn't show every extreme that they name: slot_of holds every slot once; its first 26 entries are the slots of tables 0 to 25, the rest are unused. Slot s lies on index s // 2 of wide.
All inputs are finite; a program needn't handle non-finite values.
Results may differ from a plain program's by a relative error of at most 0.0075.
Values may be sent and summed in bfloat16 or wider, within the bound.
A program may use at most 128 MiB of HBM per device.

v0:
```python
import jax
import jax.numpy as jnp
from jax import lax
from jax.sharding import PartitionSpec as P


def table_means(slot_rows, lookup_count, table_slots):
    picked = jnp.take(slot_rows, table_slots, axis=0).astype(jnp.float32)
    scaled = picked / jnp.transpose(lookup_count).astype(jnp.float32)[:, :, None]
    return jnp.transpose(scaled, (1, 0, 2)).reshape(scaled.shape[1], -1).astype(jnp.bfloat16)


def cross_forward(stacked, down, up):
    low_rank = jnp.dot(stacked, down, preferred_element_type=jnp.float32).astype(jnp.bfloat16)
    projected = jnp.dot(low_rank, up, preferred_element_type=jnp.float32)
    return (low_rank, projected)


def crossed_output(stacked, projected, bias):
    stacked_wide = stacked.astype(jnp.float32)
    return (stacked_wide * (projected + bias.astype(jnp.float32)) + stacked_wide).astype(
        jnp.bfloat16
    )


def cross_backward(stacked, upstream, lookup_count, down, up, bias, feature_index):
    low_rank, projected = cross_forward(stacked, down, up)
    stacked_wide = stacked.astype(jnp.float32)
    upstream_wide = upstream.astype(jnp.float32)
    scale_grad = upstream_wide * stacked_wide
    grad_bias = jnp.sum(scale_grad, axis=0)
    proj_grad = scale_grad.astype(jnp.bfloat16)
    over_rows = (((0,), (0,)), ((), ()))
    over_cols = (((1,), (1,)), ((), ()))
    grad_up = lax.dot_general(low_rank, proj_grad, over_rows, preferred_element_type=jnp.float32)
    low_grad = lax.dot_general(proj_grad, up, over_cols, preferred_element_type=jnp.float32).astype(
        jnp.bfloat16
    )
    grad_down = lax.dot_general(stacked, low_grad, over_rows, preferred_element_type=jnp.float32)
    input_grad = upstream_wide * (projected + bias.astype(jnp.float32)) + upstream_wide
    input_grad = input_grad + lax.dot_general(
        low_grad, down, over_cols, preferred_element_type=jnp.float32
    )
    rows = stacked.shape[0]
    dense_gradient = input_grad[:, :feature_index].astype(jnp.bfloat16)
    table_gradient = (
        input_grad[:, feature_index:].reshape(rows, -1, feature_index)
        / lookup_count.astype(jnp.float32)[:, :, None]
    )
    table_gradient = jnp.transpose(table_gradient, (1, 0, 2)).astype(jnp.bfloat16)
    return (dense_gradient, table_gradient, grad_down, grad_up, grad_bias)


def local(
    pooled_b,
    dense_output_second,
    counts_b,
    slot_of,
    stacked_a,
    upstream_a,
    counts_a,
    down_projection,
    proj_up,
    cross_layer_bias,
):
    feature_index = dense_output_second.shape[1]
    tables = counts_b.shape[1]
    table_slots = slot_of[:tables]
    arrived = lax.all_to_all(pooled_b, "wide", split_axis=1, concat_axis=0, tiled=True)
    slot_count = arrived.shape[0]
    samples = arrived.shape[2]
    down, up, bias = (
        lax.all_gather(down_projection, "wide", axis=0, tiled=True),
        lax.all_gather(proj_up, "wide", axis=1, tiled=True),
        lax.all_gather(cross_layer_bias, "wide", axis=0, tiled=True),
    )
    slot_rows = arrived.reshape(slot_count, samples, feature_index)
    stacked_b = jnp.concatenate(
        [dense_output_second, table_means(slot_rows, counts_b, table_slots)], axis=1
    )
    low_rank, projected = cross_forward(stacked_b, down, up)
    crossed_b = crossed_output(stacked_b, projected, bias)
    dense_gradient, table_gradient, grad_down, grad_up, grad_bias = cross_backward(
        stacked_a, upstream_a, counts_a, down, up, bias, feature_index
    )
    slot_selector = (
        table_slots[None, :] == jnp.arange(slot_count, dtype=jnp.int32)[:, None]
    ).astype(jnp.bfloat16)
    slot_grad = jnp.einsum(
        "qv,vxk->qxk", slot_selector, table_gradient, preferred_element_type=jnp.float32
    ).astype(jnp.bfloat16)
    returned = lax.all_to_all(
        slot_grad.reshape(slot_count, 1, samples, feature_index),
        "wide",
        split_axis=0,
        concat_axis=1,
        tiled=True,
    )
    shares = (
        lax.psum_scatter(grad_down, "wide", scatter_dimension=0, tiled=True),
        lax.psum_scatter(grad_up, "wide", scatter_dimension=1, tiled=True),
        lax.psum_scatter(grad_bias, "wide", scatter_dimension=0, tiled=True),
    )
    summed = (
        lax.psum(shares[0].astype(jnp.bfloat16), "pair").astype(jnp.float32),
        lax.psum(shares[1].astype(jnp.bfloat16), "pair").astype(jnp.float32),
        lax.psum(shares[2].astype(jnp.bfloat16), "pair").astype(jnp.float32),
    )
    return (crossed_b, dense_gradient, returned, summed[0], summed[1], summed[2])


def solution(mesh):
    return jax.shard_map(
        local,
        mesh=mesh,
        in_specs=(
            P("wide", None, "pair", None),
            P(("wide", "pair"), None),
            P(("wide", "pair"), None),
            P(),
            P(("wide", "pair"), None),
            P(("wide", "pair"), None),
            P(("wide", "pair"), None),
            P("wide", None),
            P(None, "wide"),
            P("wide"),
        ),
        out_specs=(
            P(("wide", "pair"), None),
            P(("wide", "pair"), None),
            P("wide", None, "pair", None),
            P("wide", None),
            P(None, "wide"),
            P("wide"),
        ),
        check_vma=False,
    )
```

profile of v0, /device:TPU:0, one launch (start us, length us, event | category | flops | bytes accessed | tf_op | source)
XLA Modules:
  0.0 427.8 jit_solution(16351802026620585940)
XLA Ops:
  8.7 51.4 %all-gather.5.cloned.1.call-done = bf16[512,3456]{0,1:T(8,128)(2,1)} async-done(((bf16[512,216]{0,1:T(8,128)(2,1)}), bf16[512,3456]{0,1:T(8,128)(2,1)}) %all-gather.5.cloned.1.call-update) | async-done | bytes 3538960 | tf_op jit(solution)/shard_map/all_gather | solution.py:74
  60.1 4.2 convolution_convert_fusion
  65.0 4.1 convolution_bitcast_fusion
  69.1 8.1 %copy.35 = f32[3456,512]{1,0:T(8,128)} copy(f32[3456,512]{0,1:T(8,128)} %convolution_bitcast_fusion) | data formatting | bytes 14155776
  77.3 30.9 %all-gather.3.cloned.1.call-done = bf16[3456,512]{1,0:T(8,128)(2,1)} async-done(((bf16[216,512]{1,0:T(8,128)(2,1)}), bf16[3456,512]{1,0:T(8,128)(2,1)}) %all-gather.3.cloned.1.call-update) | async-done | bytes 3538960 | tf_op jit(solution)/shard_map/all_gather | solution.py:73
  108.2 3.1 convolution_convert_fusion.1
  112.0 4.1 fusion.9
  116.1 3.2 copy.27
  119.3 4.5 %all-to-all-start = ((bf16[2,16,256,128]{3,2,0,1:T(8,128)(2,1)}), bf16[2,16,256,128]{3,2,0,1:T(8,128)(2,1)}, u32[]{:S(2)}, u32[]{:S(2)}) async-start(bf16[2,16,256,128]{3,2,0,1:T(8,128)(2,1)} %copy.27), calls=%async_computation | async-start | bytes 4194304 | tf_op jit(solution)/shard_map/all_to_all | solution.py:69
  125.3 79.6 %all-reduce = bf16[3456]{0:T(1024)(128)(2,1)} all-reduce(bf16[3456]{0:T(1024)(128)(2,1)S(1)} %dynamic-update-slice), channel_id=1, replica_groups=mesh['wide'=16,'pair'=2] {'wide'}, use_global_device_ids=true, to_apply=%add | all-reduce | flops 3456 | bytes 13824
  206.9 3.4 fusion.1
  211.5 1.7 copy-done.2
  213.3 2.1 slice.16
  215.3 5.0 %copy.30 = f32[256,3328]{0,1:T(8,128)} copy(f32[256,3328]{1,0:T(8,128)} %slice.16) | data formatting | bytes 6815744 | tf_op jit(solution)/shard_map/slice | solution.py:47
  220.4 3.6 fusion.8
  223.9 4.5 %copy.31 = bf16[26,256,128]{2,0,1:T(8,128)(2,1)} copy(bf16[26,256,128]{1,2,0:T(8,128)(2,1)} %fusion.8) | data formatting | bytes 3407872 | tf_op jit(solution)/shard_map/convert_element_type | solution.py:50
  228.4 2.3 convert_bitcast_fusion
  230.7 2.1 copy.32
  232.8 22.1 %all-to-all-start.1 = ((bf16[32,1,256,128]{3,2,1,0:T(8,128)(2,1)}), bf16[32,1,256,128]{3,2,1,0:T(8,128)(2,1)}, u32[]{:S(2)}, u32[]{:S(2)}) async-start(bf16[32,1,256,128]{3,2,1,0:T(8,128)(2,1)} %copy.32), calls=%async_computation.1 | async-start | bytes 4194304 | tf_op jit(solution)/shard_map/all_to_all | solution.py:92
  255.0 1.4 convert_element_type.79
  258.1 115.6 %all-reduce.1 = bf16[3456]{0:T(1024)(128)(2,1)S(1)} all-reduce(f32[3456]{0:T(1024)} %fusion.6), channel_id=4, replica_groups=mesh['wide'=16,'pair'=2] {'wide'}, use_global_device_ids=true, to_apply=%region_5.6.clone | all-reduce | flops 3456 | bytes 20736
  373.8 5.1 %psum.23 = bf16[216]{0:T(256)(128)(2,1)S(1)} all-reduce(bf16[216]{0:T(256)(128)(2,1)S(1)} %dynamic-slice.4), channel_id=1, replica_groups=mesh['wide'=16,'pair'=2] {'pair'}, use_global_device_ids=true, to_apply=%region_6.7 | all-reduce | flops 216 | bytes 864 | tf_op jit(solution)/shard_map/psum | solution.py:107
  380.2 2.5 gather_fusion
  383.8 1.8 copy.28
  386.9 1.5 slice.19
  388.4 1.9 copy.36
  390.3 1.7 convert_element_type.97
  392.1 6.6 %fusion.4 = bf16[256,3456]{1,0:T(8,128)(2,1)} fusion(bf16[512,3456]{0,1:T(8,128)(2,1)} %all-gather.5.cloned.1.call-done, f32[3456]{0:T(1024)S(1)} %convert_element_type.84, bf16[256,3328]{1,0:T(8,128)(2,1)S(1)} %copy.29, bf16[256,128]{1,0:T(8,128)(2,1)S(1)} %copy-done.9, bf16[3456,512]{1,0:T(8,128)(2,1)} %all-gather.3.cloned.1.call-done), kind=kOutput, calls=%fused_computation.9 | convolution fusion | flops 1822687232 | bytes 10630656 | tf_op jit(solution)/shard_map/dot_general | solution.py:15
  398.6 3.1 copy.38
  401.8 15.9 %all-reduce.5.cloned.1.call-done = (bf16[216,512]{0,1:T(8,128)(2,1)}, bf16[512,216]{0,1:T(8,128)(2,1)}) async-done(((bf16[216,512]{0,1:T(8,128)(2,1)}, bf16[512,216]{0,1:T(8,128)(2,1)}), (bf16[216,512]{0,1:T(8,128)(2,1)}, bf16[512,216]{0,1:T(8,128)(2,1)})) %all-reduce.5.cloned.1.call-update) | async-done | bytes 442384 | tf_op jit(solution)/shard_map/psum | solution.py:105
  417.7 1.7 convert_element_type.98
  419.4 1.8 copy.34
  (48 shorter events, 12.0 us)
Async XLA Ops:
  7.2 53.0 %all-gather.5.cloned.1.call-start = ((), (), s32[]{:S(2)}) async-start(), calls=%async_computation.5 | async-start | bytes 3760128 | tf_op jit(solution)/shard_map/all_gather | solution.py:74
  7.9 100.3 %all-gather.3.cloned.1.call-start = ((), (), s32[]{:S(2)}) async-start(), calls=%async_computation.4 | async-start | bytes 3760128 | tf_op jit(solution)/shard_map/all_gather | solution.py:73
  8.6 56.4 %copy-start = (bf16[256,3456]{1,0:T(8,128)(2,1)S(1)}, bf16[256,3456]{1,0:T(8,128)(2,1)}, u32[]{:S(2)}) copy-start(bf16[256,3456]{1,0:T(8,128)(2,1)} %param.14) | copy-start | bytes 5308420
  8.7 379.8 %reduce-scatter.7.cloned.1.call-start = ((), (), s32[]{:S(2)}) async-start(), calls=%async_computation.7 | async-start | bytes 7520256
  64.3 0.7 copy-start.4
  77.2 34.8 %copy-start.1 = (bf16[256,3456]{1,0:T(8,128)(2,1)S(1)}, bf16[256,3456]{1,0:T(8,128)(2,1)}, u32[]{:S(2)}) copy-start(bf16[256,3456]{1,0:T(8,128)(2,1)} %param.15) | copy-start | bytes 5308420
  77.2 313.1 %reduce-scatter.5.cloned.1.call-start = ((), (), s32[]{:S(2)}) async-start(), calls=%async_computation.6 | async-start | bytes 7520256 | tf_op jit(solution)/shard_map/reduce_scatter | solution.py:101
  111.3 0.7 copy-start.6
  116.1 7.7 %copy-start.8 = (u32[32]{0:T(128)S(1)}, u32[32]{0:T(128)}, u32[]{:S(2)}) copy-start(u32[32]{0:T(128)} %constant.24) | copy-start | bytes 388
  116.1 8.9 %copy-start.10 = (bf16[216]{0:T(256)(128)(2,1)S(1)}, bf16[216]{0:T(256)(128)(2,1)}, u32[]{:S(2)}) copy-start(bf16[216]{0:T(256)(128)(2,1)} %param.19) | copy-start | bytes 1300
  119.3 113.5 %all-to-all-start = ((bf16[2,16,256,128]{3,2,0,1:T(8,128)(2,1)}), bf16[2,16,256,128]{3,2,0,1:T(8,128)(2,1)}, u32[]{:S(2)}, u32[]{:S(2)}) async-start(bf16[2,16,256,128]{3,2,0,1:T(8,128)(2,1)} %copy.27), calls=%async_computation | async-start | bytes 4194304 | tf_op jit(solution)/shard_map/all_to_all | solution.py:69
  206.9 3.4 copy-start.3
  206.9 3.4 copy-start.5
  211.5 1.7 copy-start.2
  232.8 165.8 %all-to-all-start.1 = ((bf16[32,1,256,128]{3,2,1,0:T(8,128)(2,1)}), bf16[32,1,256,128]{3,2,1,0:T(8,128)(2,1)}, u32[]{:S(2)}, u32[]{:S(2)}) async-start(bf16[32,1,256,128]{3,2,1,0:T(8,128)(2,1)} %copy.32), calls=%async_computation.1 | async-start | bytes 4194304 | tf_op jit(solution)/shard_map/all_to_all | solution.py:92
  254.9 162.7 %all-reduce.5.cloned.1.call-start = ((), (), s32[]{:S(2)}) async-start(), calls=%async_computation.8 | async-start | bytes 966656 | tf_op jit(solution)/shard_map/psum | solution.py:105
  258.1 124.5 %copy-start.7 = (f32[256,26]{0,1:T(8,128)S(1)}, f32[256,26]{0,1:T(8,128)}, u32[]{:S(2)}) copy-start(f32[256,26]{0,1:T(8,128)} %convert_element_type.79) | copy-start | bytes 79876
  385.6 6.5 %copy-start.9 = (bf16[256,128]{1,0:T(8,128)(2,1)S(1)}, bf16[256,128]{1,0:T(8,128)(2,1)}, u32[]{:S(2)}) copy-start(bf16[256,128]{1,0:T(8,128)(2,1)} %param.11) | copy-start | bytes 196612
Sparse Core Ops, SparseCore 0:
  10.3 49.8 all-gather.4
  62.4 45.7 all-gather.2
  112.2 111.3 reduce-scatter.6
  227.4 121.7 reduce-scatter.4
  392.2 25.4 all-reduce.4
where the time goes:
time: 429 us; the launch traced here: 428 us
  blocking collectives  200 us (47%)
  waiting for transfers between devices  99.7 us (23%)
  local copies, waits for them, and re-layouts  42.9 us (10%)
  matrix products  28.8 us (7%)
  starting transfers between devices  26.8 us (6%)
  between operations  15.3 us (4%)
  other arithmetic  14 us (3%)
    unnamed x2, blocking collectives  195 us
    all_gather x1, waiting for transfers between devices, local(): lax.all_gather(proj_up, 'wide', axis=1, tiled=True)  51.4 us
    all_gather x1, waiting for transfers between devices, local(): lax.all_gather(down_projection, 'wide', axis=0, tiled=True)  30.9 us
    all_to_all x1, starting transfers between devices, local(): lax.all_to_all(slot_grad.reshape(slot_count, 1, samples, feature_index),...  22.1 us
    unnamed x30, local copies, waits for them, and re-layouts  19 us
    psum x1, waiting for transfers between devices, local(): lax.psum(shares[0].astype(jnp.bfloat16), 'pair').astype(jnp.float32)  15.9 us
    dot_general x2, matrix products, cross_forward(): projected = jnp.dot(low_rank, up, preferred_element_type=jnp.float32)  9.97 us
  transfers between devices with their start and end apart: 7, of which 3 were waited for; matrix products, arithmetic and copies ran while one was open for 18% of the time, Pallas kernels for 0%

commit v1 on v0

--- a/solution.py
+++ b/solution.py
@@ -2,6 +2,7 @@
 import jax.numpy as jnp
 from jax import lax
 from jax.sharding import PartitionSpec as P
+from jax.lax import all_gather
 
 
 def table_means(slot_rows, lookup_count, table_slots):
@@ -71,7 +72,7 @@
     samples = arrived.shape[2]
     down, up, bias = (
         lax.all_gather(down_projection, "wide", axis=0, tiled=True),
-        lax.all_gather(proj_up, "wide", axis=1, tiled=True),
+        jnp.concatenate(all_gather(proj_up, "wide"), 1),
         lax.all_gather(cross_layer_bias, "wide", axis=0, tiled=True),
     )
     slot_rows = arrived.reshape(slot_count, samples, feature_index)

time: 429 us -> 433 us (level)
  local copies, waits for them, and re-layouts: 42.9 us -> 52.5 us
    unnamed x30 -> x33, local copies, waits for them, and re-layouts: 19 us -> 23.1 us
  transfers between devices with their start and end apart: 7 -> 7, of which waited for: 3 -> 3; matrix products, arithmetic and copies ran while one was open for 18% -> 20% of each run, Pallas kernels for 0% -> 0%
where the time goes in v1:
time: 433 us; the launch traced here: 432 us
  blocking collectives  200 us (46%)
  waiting for transfers between devices  98.2 us (23%)
  local copies, waits for them, and re-layouts  52.5 us (12%)
  starting transfers between devices  26.4 us (6%)
  matrix products  25.7 us (6%)
  between operations  15.3 us (4%)
  other arithmetic  14 us (3%)
    unnamed x2, blocking collectives  195 us
    all_gather x1, waiting for transfers between devices, local(): all_gather(proj_up, 'wide')  53 us
    all_gather x1, waiting for transfers between devices, local(): lax.all_gather(down_projection, 'wide', axis=0, tiled=True)  27.5 us
    unnamed x33, local copies, waits for them, and re-layouts  23.1 us
    all_to_all x1, starting transfers between devices, local(): lax.all_to_all(slot_grad.reshape(slot_count, 1, samples, feature_index),...  21.7 us
    psum x1, waiting for transfers between devices, local(): lax.psum(shares[0].astype(jnp.bfloat16), 'pair').astype(jnp.float32)  16.3 us
    dot_general x2, matrix products, cross_forward(): projected = jnp.dot(low_rank, up, preferred_element_type=jnp.float32)  9.94 us
  transfers between devices with their start and end apart: 7, of which 3 were waited for; matrix products, arithmetic and copies ran while one was open for 20% of the time, Pallas kernels for 0%

profile of v1, /device:TPU:0, one launch (start us, length us, event | category | flops | bytes accessed | tf_op | source)
XLA Modules:
  0.0 432.3 jit_solution(3064193255996439607)
XLA Ops:
  8.7 53.0 %all-gather.6.cloned.1.call-done = bf16[8192,216]{0,1:T(8,128)(2,1)} async-done(((bf16[512,216]{0,1:T(8,128)(2,1)}), bf16[8192,216]{0,1:T(8,128)(2,1)}) %all-gather.6.cloned.1.call-update) | async-done | bytes 3538960 | tf_op jit(solution)/shard_map/all_gather | solution.py:75
  61.7 3.5 copy.46
  65.3 2.0 copy.38
  69.7 4.1 convolution_bitcast_fusion
  73.8 8.0 %copy.44 = f32[3456,512]{1,0:T(8,128)} copy(f32[3456,512]{0,1:T(8,128)} %convolution_bitcast_fusion) | data formatting | bytes 14155776
  81.9 27.5 %all-gather.4.cloned.1.call-done = bf16[3456,512]{1,0:T(8,128)(2,1)} async-done(((bf16[216,512]{1,0:T(8,128)(2,1)}), bf16[3456,512]{1,0:T(8,128)(2,1)}) %all-gather.4.cloned.1.call-update) | async-done | bytes 3538960 | tf_op jit(solution)/shard_map/all_gather | solution.py:74
  109.3 3.1 convolution_convert_fusion.1
  113.2 4.1 fusion.9
  117.3 3.2 copy.35
  120.4 4.5 %all-to-all-start = ((bf16[2,16,256,128]{3,2,0,1:T(8,128)(2,1)}), bf16[2,16,256,128]{3,2,0,1:T(8,128)(2,1)}, u32[]{:S(2)}, u32[]{:S(2)}) async-start(bf16[2,16,256,128]{3,2,0,1:T(8,128)(2,1)} %copy.35), calls=%async_computation | async-start | bytes 4194304 | tf_op jit(solution)/shard_map/all_to_all | solution.py:70
  126.4 79.6 %all-reduce = bf16[3456]{0:T(1024)(128)(2,1)} all-reduce(bf16[3456]{0:T(1024)(128)(2,1)S(1)} %dynamic-update-slice), channel_id=1, replica_groups=mesh['wide'=16,'pair'=2] {'wide'}, use_global_device_ids=true, to_apply=%add | all-reduce | flops 3456 | bytes 13824
  208.1 3.4 fusion.1
  212.7 1.8 copy-done.4
  214.4 2.1 slice.16
  216.5 5.0 %copy.39 = f32[256,3328]{0,1:T(8,128)} copy(f32[256,3328]{1,0:T(8,128)} %slice.16) | data formatting | bytes 6815744 | tf_op jit(solution)/shard_map/slice | solution.py:48
  221.5 3.6 fusion.8
  225.1 4.5 %copy.40 = bf16[26,256,128]{2,0,1:T(8,128)(2,1)} copy(bf16[26,256,128]{1,2,0:T(8,128)(2,1)} %fusion.8) | data formatting | bytes 3407872 | tf_op jit(solution)/shard_map/convert_element_type | solution.py:51
  229.6 2.3 convert_bitcast_fusion
  231.9 2.1 copy.41
  234.0 21.7 %all-to-all-start.1 = ((bf16[32,1,256,128]{3,2,1,0:T(8,128)(2,1)}), bf16[32,1,256,128]{3,2,1,0:T(8,128)(2,1)}, u32[]{:S(2)}, u32[]{:S(2)}) async-start(bf16[32,1,256,128]{3,2,1,0:T(8,128)(2,1)} %copy.41), calls=%async_computation.1 | async-start | bytes 4194304 | tf_op jit(solution)/shard_map/all_to_all | solution.py:93
  258.9 115.1 %all-reduce.1 = bf16[3456]{0:T(1024)(128)(2,1)S(1)} all-reduce(f32[3456]{0:T(1024)} %fusion.6), channel_id=5, replica_groups=mesh['wide'=16,'pair'=2] {'wide'}, use_global_device_ids=true, to_apply=%region_5.6.clone | all-reduce | flops 3456 | bytes 20736
  374.1 5.5 %psum.23 = bf16[216]{0:T(256)(128)(2,1)S(1)} all-reduce(bf16[216]{0:T(256)(128)(2,1)S(1)} %dynamic-slice.4), channel_id=1, replica_groups=mesh['wide'=16,'pair'=2] {'pair'}, use_global_device_ids=true, to_apply=%region_6.7 | all-reduce | flops 216 | bytes 864 | tf_op jit(solution)/shard_map/psum | solution.py:108
  380.8 2.5 gather_fusion
  384.4 2.7 copy.36
  387.1 3.9 copy.37
  392.6 1.9 copy.45
  394.4 1.7 convert_element_type.97
  396.2 6.6 %fusion.4 = bf16[256,3456]{1,0:T(8,128)(2,1)} fusion(bf16[512,3456]{0,1:T(8,128)(2,1)S(1)} %bitcast.52, f32[3456]{0:T(1024)S(1)} %convert_element_type.84, bf16[256,3328]{1,0:T(8,128)(2,1)} %copy.37, bf16[256,128]{1,0:T(8,128)(2,1)} %param.11, bf16[3456,512]{1,0:T(8,128)(2,1)} %all-gather.4.cloned.1.call-done), kind=kOutput, calls=%fused_computation.9 | convolution fusion | flops 1822687232 | bytes 10630656 | tf_op jit(solution)/shard_map/dot_general | solution.py:16
  402.7 3.1 copy.48
  405.9 16.3 %all-reduce.5.cloned.1.call-done = (bf16[216,512]{0,1:T(8,128)(2,1)}, bf16[512,216]{0,1:T(8,128)(2,1)}) async-done(((bf16[216,512]{0,1:T(8,128)(2,1)}, bf16[512,216]{0,1:T(8,128)(2,1)}), (bf16[216,512]{0,1:T(8,128)(2,1)}, bf16[512,216]{0,1:T(8,128)(2,1)})) %all-reduce.5.cloned.1.call-update) | async-done | bytes 442384 | tf_op jit(solution)/shard_map/psum | solution.py:106
  422.1 1.7 convert_element_type.98
  423.9 1.8 copy.43
  (52 shorter events, 15.3 us)
Async XLA Ops:
  7.2 54.6 %all-gather.6.cloned.1.call-start = ((), (), s32[]{:S(2)}) async-start(), calls=%async_computation.6 | async-start | bytes 3760128 | tf_op jit(solution)/shard_map/all_gather | solution.py:75
  7.9 101.4 %all-gather.4.cloned.1.call-start = ((), (), s32[]{:S(2)}) async-start(), calls=%async_computation.4 | async-start | bytes 3760128 | tf_op jit(solution)/shard_map/all_gather | solution.py:74
  8.6 383.9 %reduce-scatter.7.cloned.1.call-start = ((), (), s32[]{:S(2)}) async-start(), calls=%async_computation.7 | async-start | bytes 7520256
  65.2 2.0 copy-start
  65.3 2.0 copy-start.1
  67.3 1.7 copy-start.2
  69.0 0.7 copy-start.6
  81.8 312.6 %reduce-scatter.5.cloned.1.call-start = ((), (), s32[]{:S(2)}) async-start(), calls=%async_computation.5 | async-start | bytes 7520256 | tf_op jit(solution)/shard_map/reduce_scatter | solution.py:102
  112.5 0.7 copy-start.8
  117.3 7.6 %copy-start.10 = (u32[32]{0:T(128)S(1)}, u32[32]{0:T(128)}, u32[]{:S(2)}) copy-start(u32[32]{0:T(128)} %constant.24) | copy-start | bytes 388
  117.3 8.9 %copy-start.11 = (bf16[216]{0:T(256)(128)(2,1)S(1)}, bf16[216]{0:T(256)(128)(2,1)}, u32[]{:S(2)}) copy-start(bf16[216]{0:T(256)(128)(2,1)} %param.19) | copy-start | bytes 1300
  120.4 113.6 %all-to-all-start = ((bf16[2,16,256,128]{3,2,0,1:T(8,128)(2,1)}), bf16[2,16,256,128]{3,2,0,1:T(8,128)(2,1)}, u32[]{:S(2)}, u32[]{:S(2)}) async-start(bf16[2,16,256,128]{3,2,0,1:T(8,128)(2,1)} %copy.35), calls=%async_computation | async-start | bytes 4194304 | tf_op jit(solution)/shard_map/all_to_all | solution.py:70
  208.1 3.4 copy-start.5
  208.1 3.4 copy-start.7
  212.7 1.8 copy-start.4
  234.0 168.7 %all-to-all-start.1 = ((bf16[32,1,256,128]{3,2,1,0:T(8,128)(2,1)}), bf16[32,1,256,128]{3,2,1,0:T(8,128)(2,1)}, u32[]{:S(2)}, u32[]{:S(2)}) async-start(bf16[32,1,256,128]{3,2,1,0:T(8,128)(2,1)} %copy.41), calls=%async_computation.1 | async-start | bytes 4194304 | tf_op jit(solution)/shard_map/all_to_all | solution.py:93
  255.7 166.4 %all-reduce.5.cloned.1.call-start = ((), (), s32[]{:S(2)}) async-start(), calls=%async_computation.8 | async-start | bytes 966656 | tf_op jit(solution)/shard_map/psum | solution.py:106
  258.9 124.3 %copy-start.9 = (f32[256,26]{0,1:T(8,128)S(1)}, f32[256,26]{0,1:T(8,128)}, u32[]{:S(2)}) copy-start(f32[256,26]{0,1:T(8,128)} %convert_element_type.79) | copy-start | bytes 79876
  387.1 9.1 %copy-start.3 = (bf16[512,16,216]{0,2,1:T(8,128)(2,1)S(1)}, bf16[512,16,216]{0,2,1:T(8,128)(2,1)}, u32[]{:S(2)}) copy-start(bf16[512,16,216]{0,2,1:T(8,128)(2,1)} %copy-done.2) | copy-start | bytes 10616836
Sparse Core Ops, SparseCore 0:
  10.1 51.5 all-gather.5
  64.0 45.2 all-gather.3
  113.4 111.3 reduce-scatter.6
  228.6 121.7 reduce-scatter.4
  396.3 25.8 all-reduce.4
